TPU v7x, 512 devices: a whole 4x4x16 slice. The times are simulated.
512 devices in a mesh: lat: 128 (over y, z, x_hi), lon: 4 (over x_lo, core).
Axes of the slice: x: 4 (x_hi: 2, x_lo: 2; x = x_hi * 2 + x_lo), y: 4, z: 16, core: 2. Of those that a mesh axis runs over, the one named last changes fastest.
Arguments:
- grid_state: bfloat16 [256, 720, 640], P('lat', 'lon'), may hold values from -6 to 6
- conv_weight: float32 [3, 3, 640], replicated, may hold values from -2.4 to 2.4
- spectral_gain: float32 [2, 256, 640], P(None, None, 'lon'), may hold values from -4 to 4
- spectral_weight: bfloat16 [2, 640, 640], P(None, None, 'lon'), may hold values from -0.125 to 0.125
- norm_gain: float32 [640], replicated, may hold values from 0.1 to 1.9
- expand_weight: bfloat16 [640, 1280], replicated, may hold values from -0.25 to 0.25
- reduce_weight: bfloat16 [1280, 640], replicated, may hold values from -0.15625 to 0.15625
Outputs:
- block_output: bfloat16 [256, 720, 640], P('lat', 'lon')
All inputs are finite; a program needn't handle non-finite values.
Results may differ from a plain program's by a relative error of at most 0.015.
Values may be sent and summed in bfloat16 or wider, within the bound.
A program may use at most 64 MiB of HBM per device.

v0:
```python
import math
import jax
import jax.numpy as jnp
from jax import lax
from jax.sharding import PartitionSpec as P

M = 256
norm_eps = 1e-06
underflow_cut = -60.0
degree_block = 16


def padded_2(value, sides, width, wrap):
    for axis, dim in sides:
        count, length = (lax.axis_size(axis), value.shape[dim])
        up = [(i, (i + 1) % count) for i in range(count if wrap else count - 1)]
        down = [(j, i) for i, j in up]
        last = lax.slice_in_dim(value, length - width, length, axis=dim)
        initial = lax.slice_in_dim(value, 0, width, axis=dim)
        before = lax.ppermute(last, axis, up)
        after = lax.ppermute(initial, axis, down)
        value = jnp.concatenate([before, value, after], axis=dim)
    return value


def joined_along(parts, dim):
    parts = jnp.moveaxis(parts, 0, dim)
    dims = parts.shape
    return parts.reshape(*dims[:dim], dims[dim] * dims[dim + 1], *dims[dim + 2 :])


def from_everyone(value, axis):
    copies = jnp.broadcast_to(value, (lax.axis_size(axis), *value.shape))
    return lax.all_to_all(copies, axis, split_axis=0, concat_axis=0, tiled=True)


def gathered_copies(value, axis, dim):
    return joined_along(from_everyone(value, axis), dim)


def legendre_table(orders, lat_total, degree_count):
    colatitude = (jnp.arange(lat_total, dtype=jnp.float32) + 0.5) * (math.pi / lat_total)
    cosines = jnp.cos(colatitude)
    sine_values = jnp.sin(colatitude)
    rank_values = jnp.arange(1, degree_count + 1, dtype=jnp.int32)
    rank_float = rank_values.astype(jnp.float32)
    log_terms = 0.5 * jnp.log((2.0 * rank_float + 1.0) / (2.0 * rank_float))
    log_norm = jnp.sum(
        jnp.where(rank_values[None, :] <= orders[:, None], log_terms[None, :], jnp.float32(0.0)),
        axis=1,
    )
    order_float = orders.astype(jnp.float32)[:, None]
    log_start = (
        -0.5 * math.log(4.0 * math.pi)
        + log_norm[:, None]
        + order_float * jnp.log(sine_values)[None, :]
    )
    start_value = jnp.where(
        log_start > underflow_cut, jnp.exp(jnp.maximum(log_start, underflow_cut)), jnp.float32(0.0)
    )

    def advance_block(totals, block_start):
        previous, earlier = totals
        rows_out = []
        for inner in range(degree_block):
            degree = block_start + inner
            degree_float = degree.astype(jnp.float32)
            raise_coef = jnp.sqrt(
                jnp.maximum(4.0 * degree_float * degree_float - 1.0, 0.0)
                / jnp.maximum(degree_float * degree_float - order_float * order_float, 1.0)
            )
            lower_coef = jnp.sqrt(
                jnp.maximum((degree_float - 1.0) ** 2 - order_float * order_float, 0.0)
                / jnp.maximum(4.0 * (degree_float - 1.0) ** 2 - 1.0, 1.0)
            )
            recurred = raise_coef * (cosines[None, :] * previous - lower_coef * earlier)
            current = jnp.where(
                degree < orders[:, None],
                jnp.float32(0.0),
                jnp.where(degree == orders[:, None], start_value, recurred),
            )
            earlier = previous
            previous = current
            rows_out.append(current)
        return ((previous, earlier), jnp.stack(rows_out, axis=0))

    blank = jnp.zeros((orders.shape[0], lat_total), jnp.float32)
    starts = jnp.arange(0, degree_count, degree_block, dtype=jnp.int32)
    unused, table_blocks = lax.scan(advance_block, (blank, blank), starts)
    return table_blocks.reshape(degree_count, orders.shape[0], lat_total)


def quadrature(lat_total):
    colatitude = (jnp.arange(lat_total, dtype=jnp.float32) + 0.5) * (math.pi / lat_total)
    return 2.0 * math.pi * math.pi / lat_total * jnp.sin(colatitude)


def fourier_table(longitudes, lon_total, mode_count):
    mode_index = jnp.arange(mode_count, dtype=jnp.int32)
    phase_index = longitudes[:, None] * mode_index[None, :] % lon_total
    angles = phase_index.astype(jnp.float32) * (2.0 * math.pi / lon_total)
    return (jnp.stack([jnp.cos(angles), -jnp.sin(angles)], axis=1) / lon_total).astype(jnp.bfloat16)


def synthesis_table(longitudes, lon_total, mode_count):
    mode_index = jnp.arange(mode_count, dtype=jnp.int32)
    phase_index = mode_index[:, None] * longitudes[None, :] % lon_total
    angles = phase_index.astype(jnp.float32) * (2.0 * math.pi / lon_total)
    doubling = jnp.where(mode_index == 0, 1.0, 2.0).astype(jnp.float32)[:, None]
    return jnp.stack([doubling * jnp.cos(angles), -doubling * jnp.sin(angles)], axis=0).astype(
        jnp.bfloat16
    )


def shards(
    grid_state, conv_weight, spectral_gain, spectral_weight, norm_gain, expand_weight, reduce_weight
):
    lat_rows, sector_width, channel_total = grid_state.shape
    lat_count = lax.axis_size("lat")
    lon_count = lax.axis_size("lon")
    lat_total = lat_rows * lat_count
    lon_total = sector_width * lon_count
    mode_count = M
    order_share = mode_count // lat_count
    channel_share = channel_total // lon_count
    lat_position = lax.axis_index("lat")
    wrapped = padded_2(grid_state, (("lon", 1),), 1, True)
    padded = padded_2(wrapped, (("lat", 0),), 1, False)
    padded_wide = padded.astype(jnp.float32)
    filtered = jnp.zeros((lat_rows, sector_width, channel_total), jnp.float32)
    for row_shift in range(3):
        for col_shift in range(3):
            filtered = (
                filtered
                + conv_weight[row_shift, col_shift]
                * padded_wide[
                    row_shift : row_shift + lat_rows, col_shift : col_shift + sector_width
                ]
            )
    first_section = (grid_state.astype(jnp.float32) + jax.nn.gelu(filtered)).astype(jnp.bfloat16)
    gathered = lax.all_to_all(first_section, "lon", split_axis=2, concat_axis=1, tiled=True)
    forward_table = fourier_table(jnp.arange(lon_total, dtype=jnp.int32), lon_total, mode_count)
    spectrum = jnp.einsum(
        "tpc,prm->tmrc", gathered, forward_table, preferred_element_type=jnp.float32
    ).astype(jnp.bfloat16)
    cycle_spectrum = lax.all_to_all(spectrum, "lat", split_axis=1, concat_axis=0, tiled=True)
    orders = lat_position * order_share + jnp.arange(order_share, dtype=jnp.int32)
    legendre = legendre_table(orders, lat_total, mode_count)
    analysis_table = (legendre * quadrature(lat_total)[None, None, :]).astype(jnp.bfloat16)
    coefficients = jnp.einsum(
        "lmt,tmrc->lmrc", analysis_table, cycle_spectrum, preferred_element_type=jnp.float32
    )
    gain_real = spectral_gain[0][:, None, :]
    gain_imag = spectral_gain[1][:, None, :]
    coef_real = coefficients[:, :, 0, :]
    coef_imag = coefficients[:, :, 1, :]
    gained = jnp.stack(
        [
            gain_real * coef_real - gain_imag * coef_imag,
            gain_real * coef_imag + gain_imag * coef_real,
        ],
        axis=2,
    ).astype(jnp.bfloat16)
    blank = jnp.zeros((mode_count * order_share, channel_share), jnp.float32)
    portion = gathered_copies(gained, "lon", 3)
    width_part = portion.shape[3]
    weight_rows = lax.slice_in_dim(spectral_weight, 0, width_part, axis=1)
    real_part = portion[:, :, 0, :].reshape(-1, width_part)
    imag_part = portion[:, :, 1, :].reshape(-1, width_part)
    real_sum = (
        blank
        + jnp.dot(real_part, weight_rows[0], preferred_element_type=jnp.float32)
        - jnp.dot(imag_part, weight_rows[1], preferred_element_type=jnp.float32)
    )
    imag_sum = (
        blank
        + jnp.dot(real_part, weight_rows[1], preferred_element_type=jnp.float32)
        + jnp.dot(imag_part, weight_rows[0], preferred_element_type=jnp.float32)
    )
    mixed = jnp.stack(
        [
            real_sum.reshape(mode_count, order_share, channel_share),
            imag_sum.reshape(mode_count, order_share, channel_share),
        ],
        axis=2,
    ).astype(jnp.bfloat16)
    synthesis_legendre = legendre.astype(jnp.bfloat16)
    cycle_modes = jnp.einsum(
        "lmt,lmrc->tmrc", synthesis_legendre, mixed, preferred_element_type=jnp.float32
    ).astype(jnp.bfloat16)
    band_modes = lax.all_to_all(cycle_modes, "lat", split_axis=0, concat_axis=1, tiled=True)
    inverse_table = synthesis_table(jnp.arange(lon_total, dtype=jnp.int32), lon_total, mode_count)
    all_lons = jnp.einsum(
        "tmrc,rmp->tpc", band_modes, inverse_table, preferred_element_type=jnp.float32
    )
    spectral_out = lax.all_to_all(
        all_lons.astype(jnp.bfloat16), "lon", split_axis=1, concat_axis=2, tiled=True
    ).astype(all_lons.dtype)
    second_section = (first_section.astype(jnp.float32) + spectral_out).astype(jnp.bfloat16)
    second_wide = second_section.astype(jnp.float32)
    scale_values = lax.rsqrt(jnp.mean(second_wide * second_wide, axis=-1, keepdims=True) + norm_eps)
    normed = (second_wide * norm_gain * scale_values).astype(jnp.bfloat16)
    flat_rows = normed.reshape(-1, channel_total)
    hidden = jax.nn.gelu(
        jnp.dot(flat_rows, expand_weight, preferred_element_type=jnp.float32)
    ).astype(jnp.bfloat16)
    update = jnp.dot(hidden, reduce_weight, preferred_element_type=jnp.float32)
    block_output = (second_wide.reshape(-1, channel_total) + update).astype(jnp.bfloat16)
    return block_output.reshape(lat_rows, sector_width, channel_total)


def solution(mesh):
    return jax.shard_map(
        shards,
        mesh=mesh,
        in_specs=(
            P("lat", "lon", None),
            P(),
            P(None, None, "lon"),
            P(None, None, "lon"),
            P(),
            P(),
            P(),
        ),
        out_specs=P("lat", "lon", None),
        check_vma=False,
    )
```

profile of v0, /device:TPU:1, one launch (start us, length us, event | category | flops | bytes accessed | tf_op | source)
XLA Modules:
  0.0 384.5 jit_solution(18043150537942124979)
XLA Ops:
  1.2 4.5 %collective-permute-start = (bf16[2,1,640]{2,1,0:T(2,128)(2,1)S(1)}, bf16[2,1,640]{2,1,0:T(2,128)(2,1)S(1)}, u32[]{:S(2)}, u32[]{:S(2)}) collective-permute-start(bf16[2,1,640]{2,1,0:T(2,128)(2,1)S(1)} %get-tuple-element.533), channel_id=1, source_target_pairs={{0,1},{1,2},{2,3},{3,0},{4,5},{5,6},{6,7},{7,4},{8,9},{9,10},{10,1... | collective-permute-start | bytes 7688 | tf_op jit(solution)/shard_map/ppermute | solution.py:20
  5.7 6.2 %collective-permute-start.1 = (bf16[2,1,640]{2,1,0:T(2,128)(2,1)S(1)}, bf16[2,1,640]{2,1,0:T(2,128)(2,1)S(1)}, u32[]{:S(2)}, u32[]{:S(2)}) collective-permute-start(bf16[2,1,640]{2,1,0:T(2,128)(2,1)S(1)} %get-tuple-element.534), channel_id=1, source_target_pairs={{1,0},{2,1},{3,2},{0,3},{5,4},{6,5},{7,6},{4,7},{9,8},{10,9},{11,1... | collective-permute-start | bytes 7688 | tf_op jit(solution)/shard_map/ppermute | solution.py:21
  13.1 2.1 collective-permute-start.2
  15.2 1.3 collective-permute-start.3
  16.5 4.3 %sine_negate_fusion = (f32[720,1,256]{2,0,1:T(8,128)}, f32[720,1,256]{2,0,1:T(8,128)}) fusion(), kind=kLoop, calls=%fused_computation.182 | loop fusion | flops 1843200 | bytes 1474560 | tf_op jit(solution)/shard_map/neg | solution.py:102
  20.8 3.9 %collective-permute-done.3 = bf16[1,182,640]{2,1,0:T(8,128)(2,1)S(1)} collective-permute-done((bf16[1,182,640]{2,1,0:T(8,128)(2,1)S(1)}, bf16[1,182,640]{2,1,0:T(8,128)(2,1)S(1)}, u32[]{:S(2)}, u32[]{:S(2)}) %collective-permute-start.3) | collective-permute-done | bytes 232992 | tf_op jit(solution)/shard_map/ppermute | solution.py:21
  26.0 1.8 copy.70
  27.7 10.6 %all-to-all-start = ((bf16[2,180,640]{1,0,2:T(2,128)(2,1)}), bf16[2,180,640]{1,0,2:T(2,128)(2,1)S(1)}, u32[]{:S(2)}, u32[]{:S(2)}) async-start(bf16[2,180,640]{1,0,2:T(2,128)(2,1)} %copy.70), calls=%async_computation | async-start | bytes 1310720 | tf_op jit(solution)/shard_map/all_to_all | solution.py:141
  38.5 9.1 %all-to-all-done = bf16[2,180,640]{1,0,2:T(2,128)(2,1)S(1)} async-done(((bf16[2,180,640]{1,0,2:T(2,128)(2,1)}), bf16[2,180,640]{1,0,2:T(2,128)(2,1)S(1)}, u32[]{:S(2)}, u32[]{:S(2)}) %all-to-all-start) | async-done | bytes 460832 | tf_op jit(solution)/shard_map/all_to_all | solution.py:141
  48.6 1.8 fusion.56
  51.5 16.9 %all-to-all-start.1 = ((bf16[2,256,2,160]{3,0,2,1:T(2,128)(2,1)}), bf16[2,256,2,160]{3,0,2,1:T(2,128)(2,1)S(1)}, u32[]{:S(2)}, u32[]{:S(2)}) async-start(bf16[2,256,2,160]{3,0,2,1:T(2,128)(2,1)} %copy.73), calls=%async_computation.1 | async-start | bytes 1048576 | tf_op jit(solution)/shard_map/all_to_all | solution.py:146
  68.4 201.7 %while.21 = (s32[]{:T(128)}, f32[2,256]{1,0:T(2,128)S(1)}, f32[2,256]{1,0:T(2,128)S(1)}, f32[16,16,2,256]{3,2,1,0:T(2,128)S(1)}, s32[16]{0:T(128)S(1)}, /*index=...) while((s32[]{:T(128)}, f32[2,256]{1,0:T(2,128)S(1)}, ...), condition=%wide.region_2.3_spmd.clone.clone.clone.clone, body=%wide.region_1.2_spmd.clone.clone.clone.clone.sunk | while | flops 92737 | bytes 279792 | solution.py:89
  271.3 19.9 %all_to_all.68 = bf16[4,256,2,2,160]{1,4,3,2,0:T(8,128)(2,1)S(1)} all-to-all(bf16[4,256,2,2,160]{1,4,3,2,0:T(8,128)(2,1)S(1)} %broadcast_in_dim.453), channel_id=1, replica_groups=mesh['lat'=128,'lon'=4] {'lon'}, dimensions={0} | all-to-all | bytes 2621440 | tf_op jit(solution)/shard_map/all_to_all | solution.py:34
  291.4 1.8 copy.79
  293.2 2.1 reshape_squeeze.6
  298.9 1.4 fusion.57
  305.6 18.3 %all-to-all-start.3 = ((bf16[256,2,2,160]{3,2,1,0:T(2,128)(2,1)}), bf16[256,2,2,160]{3,2,1,0:T(2,128)(2,1)S(1)}, u32[]{:S(2)}, u32[]{:S(2)}) async-start(bf16[256,2,2,160]{3,2,1,0:T(2,128)(2,1)} %copy.86), calls=%async_computation.3 | async-start | bytes 1048576 | tf_op jit(solution)/shard_map/all_to_all | solution.py:191
  324.0 4.1 %multiply_convert_fusion.1 = (bf16[1,256,720]{1,2,0:T(8,128)(2,1)S(1)}, bf16[1,256,720]{1,2,0:T(8,128)(2,1)}) fusion(f32[256]{0:T(256)S(1)} %fusion.123, f32[256]{0:T(256)S(1)} %compare_select_fusion.2), kind=kLoop, calls=%fused_computation.187 | loop fusion | flops 2396160 | bytes 739328 | tf_op jit(solution)/shard_map/convert.10
  328.1 27.1 %all-to-all-done.3 = bf16[256,2,2,160]{3,2,1,0:T(2,128)(2,1)S(1)} async-done(((bf16[256,2,2,160]{3,2,1,0:T(2,128)(2,1)}), bf16[256,2,2,160]{3,2,1,0:T(2,128)(2,1)S(1)}, u32[]{:S(2)}, u32[]{:S(2)}) %all-to-all-start.3) | async-done | bytes 327712 | tf_op jit(solution)/shard_map/all_to_all | solution.py:191
  355.5 1.5 fusion.54
  358.0 16.8 %all_to_all.69 = bf16[2,720,160]{2,0,1:T(2,128)(2,1)S(1)} all-to-all(bf16[2,720,160]{2,0,1:T(2,128)(2,1)S(1)} %copy.89), channel_id=1, replica_groups=mesh['lat'=128,'lon'=4] {'lon'}, dimensions={1} | all-to-all | bytes 921600 | tf_op jit(solution)/shard_map/all_to_all | solution.py:196
  375.1 1.9 reshape.1013
  377.0 1.5 multiply_reduce_fusion
  379.8 3.4 fusion.53
  (891 shorter events, 68.2 us)
Async XLA Ops:
  0.0 379.8 %copy-start = (bf16[1280,640]{1,0:T(8,128)(2,1)S(1)}, bf16[1280,640]{1,0:T(8,128)(2,1)}, u32[]{:S(2)}) copy-start(bf16[1280,640]{1,0:T(8,128)(2,1)} %param.15) | copy-start | bytes 4915204
  1.2 11.7 %collective-permute-start = (bf16[2,1,640]{2,1,0:T(2,128)(2,1)S(1)}, bf16[2,1,640]{2,1,0:T(2,128)(2,1)S(1)}, u32[]{:S(2)}, u32[]{:S(2)}) collective-permute-start(bf16[2,1,640]{2,1,0:T(2,128)(2,1)S(1)} %get-tuple-element.533), channel_id=1, source_target_pairs={{0,1},{1,2},{2,3},{3,0},{4,5},{5,6},{6,7},{7,4},{8,9},{9,10},{10,1... | collective-permute-start | bytes 7688 | tf_op jit(solution)/shard_map/ppermute | solution.py:20
  5.7 7.2 %collective-permute-start.1 = (bf16[2,1,640]{2,1,0:T(2,128)(2,1)S(1)}, bf16[2,1,640]{2,1,0:T(2,128)(2,1)S(1)}, u32[]{:S(2)}, u32[]{:S(2)}) collective-permute-start(bf16[2,1,640]{2,1,0:T(2,128)(2,1)S(1)} %get-tuple-element.534), channel_id=1, source_target_pairs={{1,0},{2,1},{3,2},{0,3},{5,4},{6,5},{7,6},{4,7},{9,8},{10,9},{11,1... | collective-permute-start | bytes 7688 | tf_op jit(solution)/shard_map/ppermute | solution.py:21
  13.1 7.7 %collective-permute-start.2 = (bf16[1,182,640]{2,1,0:T(8,128)(2,1)S(1)}, bf16[1,182,640]{2,1,0:T(8,128)(2,1)S(1)}, u32[]{:S(2)}, u32[]{:S(2)}) collective-permute-start(bf16[1,182,640]{2,1,0:T(8,128)(2,1)S(1)} %get-tuple-element.531), channel_id=1, source_target_pairs={{0,4},{4,8},{8,12},{12,16},{16,20},{20,24},{24,28},{28,32},{32,36}... | collective-permute-start | bytes 698888 | tf_op jit(solution)/shard_map/ppermute | solution.py:20
  15.2 9.5 %collective-permute-start.3 = (bf16[1,182,640]{2,1,0:T(8,128)(2,1)S(1)}, bf16[1,182,640]{2,1,0:T(8,128)(2,1)S(1)}, u32[]{:S(2)}, u32[]{:S(2)}) collective-permute-start(bf16[1,182,640]{2,1,0:T(8,128)(2,1)S(1)} %get-tuple-element.532), channel_id=1, source_target_pairs={{4,0},{8,4},{12,8},{16,12},{20,16},{24,20},{28,24},{32,28},{36,32}... | collective-permute-start | bytes 698888 | tf_op jit(solution)/shard_map/ppermute | solution.py:21
  16.5 8.3 %copy-start.2 = (bf16[2,180,640]{2,0,1:T(2,128)(2,1)S(1)}, bf16[2,180,640]{2,0,1:T(2,128)(2,1)}, u32[]{:S(2)}) copy-start(bf16[2,180,640]{2,0,1:T(2,128)(2,1)} %param.9) | copy-start | bytes 1382404
  25.9 22.1 %copy-start.1 = (bf16[2,180,640]{2,1,0:T(8,128)(2,1)}, bf16[2,180,640]{2,1,0:T(8,128)(2,1)S(1)}, u32[]{:S(2)}) copy-start(bf16[2,180,640]{2,1,0:T(8,128)(2,1)S(1)} %fusion.67) | copy-start | bytes 1382404
  27.7 19.8 %all-to-all-start = ((bf16[2,180,640]{1,0,2:T(2,128)(2,1)}), bf16[2,180,640]{1,0,2:T(2,128)(2,1)S(1)}, u32[]{:S(2)}, u32[]{:S(2)}) async-start(bf16[2,180,640]{1,0,2:T(2,128)(2,1)} %copy.70), calls=%async_computation | async-start | bytes 1310720 | tf_op jit(solution)/shard_map/all_to_all | solution.py:141
  48.5 19.9 %copy-start.5 = (f32[16,16,2,256]{3,2,1,0:T(2,128)S(1)}, f32[16,16,2,256]{3,2,1,0:T(2,128)}, u32[]{:S(2)}) copy-start(f32[16,16,2,256]{3,2,1,0:T(2,128)} %custom-call.3) | copy-start | bytes 1572868
  51.5 218.7 %all-to-all-start.1 = ((bf16[2,256,2,160]{3,0,2,1:T(2,128)(2,1)}), bf16[2,256,2,160]{3,0,2,1:T(2,128)(2,1)S(1)}, u32[]{:S(2)}, u32[]{:S(2)}) async-start(bf16[2,256,2,160]{3,0,2,1:T(2,128)(2,1)} %copy.73), calls=%async_computation.1 | async-start | bytes 1048576 | tf_op jit(solution)/shard_map/all_to_all | solution.py:146
  68.4 201.8 %copy-start.7 = (f32[2,256,160]{1,2,0:T(8,128)S(1)}, f32[2,256,160]{1,2,0:T(8,128)}, u32[]{:S(2)}) copy-start(f32[2,256,160]{1,2,0:T(8,128)} %param.11) | copy-start | bytes 983044
  270.1 1.0 copy-start.6
  291.3 3.9 %copy-start.3 = (bf16[2,640,160]{1,2,0:T(8,128)(2,1)S(1)}, bf16[2,640,160]{1,2,0:T(8,128)(2,1)}, u32[]{:S(2)}) copy-start(bf16[2,640,160]{1,2,0:T(8,128)(2,1)} %param.12) | copy-start | bytes 1228804
  298.8 3.5 copy-start.4
  305.6 49.5 %all-to-all-start.3 = ((bf16[256,2,2,160]{3,2,1,0:T(2,128)(2,1)}), bf16[256,2,2,160]{3,2,1,0:T(2,128)(2,1)S(1)}, u32[]{:S(2)}, u32[]{:S(2)}) async-start(bf16[256,2,2,160]{3,2,1,0:T(2,128)(2,1)} %copy.86), calls=%async_computation.3 | async-start | bytes 1048576 | tf_op jit(solution)/shard_map/all_to_all | solution.py:191
  377.0 2.6 copy-start.8
where the time goes:
time: 387 us; the launch traced here: 384 us
  loops' own time  154 us (40%)
  starting transfers between devices  59.8 us (15%)
  other arithmetic  50.4 us (13%)
  waiting for transfers between devices  40.1 us (10%)
  blocking collectives  36.7 us (9%)
  local copies, waits for them, and re-layouts  31.1 us (8%)
  matrix products  12.2 us (3%)
    another operation x1, loops' own time, legendre_table(): unused, table_blocks = lax.scan(advance_block, (blank, blank), starts)  154 us
    all_to_all x1, waiting for transfers between devices, shards(): lax.all_to_all(cycle_modes, 'lat', split_axis=0, concat_axis=1, tiled=True)  27.1 us
    while x240, other arithmetic  21 us
    all_to_all x1, blocking collectives, from_everyone(): return lax.all_to_all(copies, axis, split_axis=0, concat_axis=0, tiled=True)  19.9 us
    all_to_all x1, starting transfers between devices, shards(): lax.all_to_all(cycle_modes, 'lat', split_axis=0, concat_axis=1, tiled=True)  18.3 us
    all_to_all x1, starting transfers between devices, shards(): lax.all_to_all(spectrum, 'lat', split_axis=1, concat_axis=0, tiled=True)  16.9 us
    all_to_all x1, blocking collectives, shards(): lax.all_to_all(all_lons.astype(jnp.bfloat16), 'lon', split_axis=1, concat...  16.8 us
    eq x256, other arithmetic, advance_block(): degree == orders[:, None]  11.4 us
  transfers between devices with their start and end apart: 7, of which 3 were waited for; matrix products, arithmetic and copies ran while one was open for 15% of the time, Pallas kernels for 0%

commit v1 on v0

--- a/solution.py
+++ b/solution.py
@@ -188,7 +188,12 @@
     cycle_modes = jnp.einsum(
         "lmt,lmrc->tmrc", synthesis_legendre, mixed, preferred_element_type=jnp.float32
     ).astype(jnp.bfloat16)
-    band_modes = lax.all_to_all(cycle_modes, "lat", split_axis=0, concat_axis=1, tiled=True)
+    band_modes = jnp.concatenate(
+        lax.all_to_all(
+            jnp.stack(jnp.split(cycle_modes, lax.axis_size("lat"), axis=0)), "lat", 0, 0
+        ),
+        axis=1,
+    )
     inverse_table = synthesis_table(jnp.arange(lon_total, dtype=jnp.int32), lon_total, mode_count)
     all_lons = jnp.einsum(
         "tmrc,rmp->tpc", band_modes, inverse_table, preferred_element_type=jnp.float32

time: 387 us -> 533 us (1.38)
  local copies, waits for them, and re-layouts: 31.1 us -> 158 us
  loops' own time: 154 us -> 166 us
    unnamed x19 -> x134, local copies, waits for them, and re-layouts: 1.24 us -> 99.8 us
    another operation x2 -> x4, local copies, waits for them, and re-layouts: 0.27 us -> 19.3 us  [the longest x2 19 us: shards(): jnp.stack(jnp.split(cycle_modes, lax.axis_size('lat'), axis=0))]
    another operation x1, loops' own time: 154 us -> 166 us  [legendre_table(): unused, table_blocks = lax.scan(advance_block, (blank, blank), starts)]
    dynamic_update_slice x16, local copies, waits for them, and re-layouts: 0.2 us -> 9.78 us  [legendre_table(): unused, table_blocks = lax.scan(advance_block, (blank, blank), starts)]
  transfers between devices with their start and end apart: 7 -> 7, of which waited for: 3 -> 3; matrix products, arithmetic and copies ran while one was open for 15% -> 13% of each run, Pallas kernels for 0% -> 0%
where the time goes in v1:
time: 533 us; the launch traced here: 529 us
  loops' own time  166 us (31%)
  local copies, waits for them, and re-layouts  158 us (30%)
  starting transfers between devices  60 us (11%)
  other arithmetic  52.2 us (10%)
  waiting for transfers between devices  40.1 us (8%)
  blocking collectives  36.7 us (7%)
  matrix products  15.4 us (3%)
    another operation x1, loops' own time, legendre_table(): unused, table_blocks = lax.scan(advance_block, (blank, blank), starts)  166 us
    unnamed x134, local copies, waits for them, and re-layouts  99.8 us
    all_to_all x1, waiting for transfers between devices, shards(): lax.all_to_all(jnp.stack(jnp.split(cycle_modes, lax.axis_size('lat'), axi...  27.1 us
    while x240, other arithmetic  21 us
    all_to_all x1, blocking collectives, from_everyone(): return lax.all_to_all(copies, axis, split_axis=0, concat_axis=0, tiled=True)  19.9 us
    another operation x2, local copies, waits for them, and re-layouts, shards(): jnp.stack(jnp.split(cycle_modes, lax.axis_size('lat'), axis=0))  19 us
    all_to_all x1, starting transfers between devices, shards(): lax.all_to_all(jnp.stack(jnp.split(cycle_modes, lax.axis_size('lat'), axi...  18.5 us
    all_to_all x1, starting transfers between devices, shards(): lax.all_to_all(spectrum, 'lat', split_axis=1, concat_axis=0, tiled=True)  16.9 us
  transfers between devices with their start and end apart: 7, of which 3 were waited for; matrix products, arithmetic and copies ran while one was open for 13% of the time, Pallas kernels for 0%

profile of v1, /device:TPU:1, one launch (start us, length us, event | category | flops | bytes accessed | tf_op | source)
XLA Modules:
  0.0 529.1 jit_solution(14343557031702392571)
XLA Ops:
  1.2 4.5 collective-permute-start
  5.7 6.2 %collective-permute-start.1 = (bf16[2,1,640]{2,1,0:T(2,128)(2,1)S(1)}, bf16[2,1,640]{2,1,0:T(2,128)(2,1)S(1)}, u32[]{:S(2)}, u32[]{:S(2)}) collective-permute-start(bf16[2,1,640]{2,1,0:T(2,128)(2,1)S(1)} %get-tuple-element.534), channel_id=1, source_target_pairs={{1,0},{2,1},{3,2},{0,3},{5,4},{6,5},{7,6},{4,7},{9,8},{10,9},{11,1... | collective-permute-start | bytes 7688 | tf_op jit(solution)/shard_map/ppermute | solution.py:21
  13.1 2.1 collective-permute-start.2
  16.5 4.2 sine_negate_fusion
  20.8 3.9 collective-permute-done.3
  24.8 2.1 fusion.67
  27.0 1.8 copy.349
  28.8 10.6 %all-to-all-start = ((bf16[2,180,640]{1,0,2:T(2,128)(2,1)}), bf16[2,180,640]{1,0,2:T(2,128)(2,1)S(1)}, u32[]{:S(2)}, u32[]{:S(2)}) async-start(bf16[2,180,640]{1,0,2:T(2,128)(2,1)} %copy.349), calls=%async_computation | async-start | bytes 1310720 | tf_op jit(solution)/shard_map/all_to_all | solution.py:141
  39.6 9.1 %all-to-all-done = bf16[2,180,640]{1,0,2:T(2,128)(2,1)S(1)} async-done(((bf16[2,180,640]{1,0,2:T(2,128)(2,1)}), bf16[2,180,640]{1,0,2:T(2,128)(2,1)S(1)}, u32[]{:S(2)}, u32[]{:S(2)}) %all-to-all-start) | async-done | bytes 460832 | tf_op jit(solution)/shard_map/all_to_all | solution.py:141
  49.6 1.8 fusion.56
  52.5 16.9 %all-to-all-start.1 = ((bf16[2,256,2,160]{3,0,2,1:T(2,128)(2,1)}), bf16[2,256,2,160]{3,0,2,1:T(2,128)(2,1)S(1)}, u32[]{:S(2)}, u32[]{:S(2)}) async-start(bf16[2,256,2,160]{3,0,2,1:T(2,128)(2,1)} %copy.352), calls=%async_computation.1 | async-start | bytes 1048576 | tf_op jit(solution)/shard_map/all_to_all | solution.py:146
  69.4 226.0 %while.21 = (s32[]{:T(128)}, f32[2,256]{1,0:T(2,128)S(1)}, f32[2,256]{1,0:T(2,128)S(1)}, f32[16,16,2,256]{3,2,1,0:T(2,128)}, s32[16]{0:T(128)S(1)}, /*index=5*/s...) while((s32[]{:T(128)}, f32[2,256]{1,0:T(2,128)S(1)}, ...), condition=%wide.region_2.3_spmd.clone.clone.clone.clone, body=%wide.region_1.2_spmd.clone.clone.clone.clone.sunk | while | flops 92737 | bytes 280300 | solution.py:89
  298.5 19.9 %all_to_all.55 = bf16[4,256,2,2,160]{1,4,3,2,0:T(8,128)(2,1)S(1)} all-to-all(bf16[4,256,2,2,160]{1,4,3,2,0:T(8,128)(2,1)S(1)} %broadcast_in_dim.453), channel_id=1, replica_groups=mesh['lat'=128,'lon'=4] {'lon'}, dimensions={0} | all-to-all | bytes 2621440 | tf_op jit(solution)/shard_map/all_to_all | solution.py:34
  318.6 1.8 copy.358
  320.4 2.1 reshape_squeeze.6
  322.5 2.0 fusion.112
  431.8 18.2 %copy.365 = bf16[128,2,2,2,160]{4,3,2,1,0:T(2,128)(2,1)} copy(bf16[128,2,2,2,160]{1,4,3,2,0:T(8,128)(2,1)} %constant_dynamic-update-slice_fusion.16) | data formatting | bytes 655360 | tf_op jit(solution)/shard_map/stack | solution.py:193
  450.0 18.5 %all-to-all-start.3 = ((bf16[128,2,2,2,160]{4,3,2,1,0:T(2,128)(2,1)}), bf16[128,2,2,2,160]{4,3,2,1,0:T(2,128)(2,1)S(1)}, u32[]{:S(2)}, u32[]{:S(2)}) async-start(bf16[128,2,2,2,160]{4,3,2,1,0:T(2,128)(2,1)} %copy.365), calls=%async_computation.3 | async-start | bytes 1048576 | tf_op jit(solution)/shard_map/all_to_all | solution.py:192
  468.6 4.1 multiply_convert_fusion.1
  472.6 27.1 %all-to-all-done.3 = bf16[128,2,2,2,160]{4,3,2,1,0:T(2,128)(2,1)S(1)} async-done(((bf16[128,2,2,2,160]{4,3,2,1,0:T(2,128)(2,1)}), bf16[128,2,2,2,160]{4,3,2,1,0:T(2,128)(2,1)S(1)}, u32[]{:S(2)}, u32[]{:S(2)}) %all-to-all-start.3) | async-done | bytes 327712 | tf_op jit(solution)/shard_map/all_to_all | solution.py:192
  502.6 16.8 %all_to_all.56 = bf16[2,720,160]{2,0,1:T(2,128)(2,1)S(1)} all-to-all(bf16[2,720,160]{2,0,1:T(2,128)(2,1)S(1)} %copy.368), channel_id=1, replica_groups=mesh['lat'=128,'lon'=4] {'lon'}, dimensions={1} | all-to-all | bytes 921600 | tf_op jit(solution)/shard_map/all_to_all | solution.py:201
  519.7 1.9 reshape.1021
  521.7 1.5 multiply_reduce_fusion
  524.5 3.4 fusion.53
  (1007 shorter events, 181.6 us)
Async XLA Ops:
  0.0 524.4 %copy-start = (bf16[1280,640]{1,0:T(8,128)(2,1)S(1)}, bf16[1280,640]{1,0:T(8,128)(2,1)}, u32[]{:S(2)}) copy-start(bf16[1280,640]{1,0:T(8,128)(2,1)} %param.15) | copy-start | bytes 4915204
  1.2 11.7 %collective-permute-start = (bf16[2,1,640]{2,1,0:T(2,128)(2,1)S(1)}, bf16[2,1,640]{2,1,0:T(2,128)(2,1)S(1)}, u32[]{:S(2)}, u32[]{:S(2)}) collective-permute-start(bf16[2,1,640]{2,1,0:T(2,128)(2,1)S(1)} %get-tuple-element.533), channel_id=1, source_target_pairs={{0,1},{1,2},{2,3},{3,0},{4,5},{5,6},{6,7},{7,4},{8,9},{9,10},{10,1... | collective-permute-start | bytes 7688 | tf_op jit(solution)/shard_map/ppermute | solution.py:20
  5.7 7.2 %collective-permute-start.1 = (bf16[2,1,640]{2,1,0:T(2,128)(2,1)S(1)}, bf16[2,1,640]{2,1,0:T(2,128)(2,1)S(1)}, u32[]{:S(2)}, u32[]{:S(2)}) collective-permute-start(bf16[2,1,640]{2,1,0:T(2,128)(2,1)S(1)} %get-tuple-element.534), channel_id=1, source_target_pairs={{1,0},{2,1},{3,2},{0,3},{5,4},{6,5},{7,6},{4,7},{9,8},{10,9},{11,1... | collective-permute-start | bytes 7688 | tf_op jit(solution)/shard_map/ppermute | solution.py:21
  13.1 7.6 %collective-permute-start.2 = (bf16[1,182,640]{2,1,0:T(8,128)(2,1)S(1)}, bf16[1,182,640]{2,1,0:T(8,128)(2,1)S(1)}, u32[]{:S(2)}, u32[]{:S(2)}) collective-permute-start(bf16[1,182,640]{2,1,0:T(8,128)(2,1)S(1)} %get-tuple-element.531), channel_id=1, source_target_pairs={{0,4},{4,8},{8,12},{12,16},{16,20},{20,24},{24,28},{28,32},{32,36}... | collective-permute-start | bytes 698888 | tf_op jit(solution)/shard_map/ppermute | solution.py:20
  15.2 9.5 %collective-permute-start.3 = (bf16[1,182,640]{2,1,0:T(8,128)(2,1)S(1)}, bf16[1,182,640]{2,1,0:T(8,128)(2,1)S(1)}, u32[]{:S(2)}, u32[]{:S(2)}) collective-permute-start(bf16[1,182,640]{2,1,0:T(8,128)(2,1)S(1)} %get-tuple-element.532), channel_id=1, source_target_pairs={{4,0},{8,4},{12,8},{16,12},{20,16},{24,20},{28,24},{32,28},{36,32}... | collective-permute-start | bytes 698888 | tf_op jit(solution)/shard_map/ppermute | solution.py:21
  27.0 42.4 %copy-start.1 = (bf16[2,180,640]{2,1,0:T(8,128)(2,1)}, bf16[2,180,640]{2,1,0:T(8,128)(2,1)S(1)}, u32[]{:S(2)}) copy-start(bf16[2,180,640]{2,1,0:T(8,128)(2,1)S(1)} %fusion.67) | copy-start | bytes 1382404
  28.8 19.8 %all-to-all-start = ((bf16[2,180,640]{1,0,2:T(2,128)(2,1)}), bf16[2,180,640]{1,0,2:T(2,128)(2,1)S(1)}, u32[]{:S(2)}, u32[]{:S(2)}) async-start(bf16[2,180,640]{1,0,2:T(2,128)(2,1)} %copy.349), calls=%async_computation | async-start | bytes 1310720 | tf_op jit(solution)/shard_map/all_to_all | solution.py:141
  52.5 243.9 %all-to-all-start.1 = ((bf16[2,256,2,160]{3,0,2,1:T(2,128)(2,1)}), bf16[2,256,2,160]{3,0,2,1:T(2,128)(2,1)S(1)}, u32[]{:S(2)}, u32[]{:S(2)}) async-start(bf16[2,256,2,160]{3,0,2,1:T(2,128)(2,1)} %copy.352), calls=%async_computation.1 | async-start | bytes 1048576 | tf_op jit(solution)/shard_map/all_to_all | solution.py:146
  423.2 101.0 %copy-start.2 = (f32[640]{0:T(1024)S(1)}, f32[640]{0:T(1024)}, u32[]{:S(2)}) copy-start(f32[640]{0:T(1024)} %param.13) | copy-start | bytes 7684
  450.0 49.8 %all-to-all-start.3 = ((bf16[128,2,2,2,160]{4,3,2,1,0:T(2,128)(2,1)}), bf16[128,2,2,2,160]{4,3,2,1,0:T(2,128)(2,1)S(1)}, u32[]{:S(2)}, u32[]{:S(2)}) async-start(bf16[128,2,2,2,160]{4,3,2,1,0:T(2,128)(2,1)} %copy.365), calls=%async_computation.3 | async-start | bytes 1048576 | tf_op jit(solution)/shard_map/all_to_all | solution.py:192
